TPU v7x, 256 devices: a whole 4x4x8 slice. The times are simulated.
256 devices in a mesh: blk: 128 (over x, z, y_hi, core), rep: 2 (over y_lo).
Axes of the slice: x: 4, y: 4 (y_hi: 2, y_lo: 2; y = y_hi * 2 + y_lo), z: 8, core: 2. Of those that a mesh axis runs over, the one named last changes fastest.
Arguments:
- frames: bfloat16 [2, 6144, 384], P('rep', 'blk'), may hold values from -600 to 600
- codebook: bfloat16 [131072, 384], P('blk'), may hold values from -2 to 2
Outputs:
- log_total: float32 [2, 6144], P('rep', 'blk')
- counts: float32 [131072], P('blk')
- entropy: float32 [], replicated
All inputs are finite; a program needn't handle non-finite values.
Results may differ from a plain program's by a relative error of at most 0.00065.
Values may be sent and summed in bfloat16 or wider, within the bound.
No kernel may reach another device: no remote copies, remote signals or barrier semaphores. Data moves between devices by JAX's collectives and lax.ppermute only.
A program may use at most 128 MiB of HBM per device.

v0:
```python
import functools
import jax
import jax.numpy as jnp
from jax import lax
from jax.sharding import Mesh
from jax.sharding import PartitionSpec as P

BLK = ("blk_0", "blk_1", "blk_2", "blk_3")


def gathered_once(array, axis):
    leaves = jax.tree.leaves(array)
    sequence = sorted(range(len(leaves)), key=lambda k: -leaves[k].size)
    width = (1, *leaves[sequence[0]].shape)[-1]
    lines = [
        jnp.pad(leaves[k].reshape(-1), (0, -leaves[k].size % width)).reshape(-1, width)
        for k in sequence
    ]
    both, at, found = (lax.all_gather(jnp.concatenate(lines), axis), 0, {})
    for k, line in zip(sequence, lines):
        slab = both[:, at : at + len(line)].reshape(len(both), -1)
        found[k] = slab[:, : leaves[k].size].reshape(-1, *leaves[k].shape)
        at += len(line)
    numbers = iter(range(len(leaves)))
    return jax.tree.map(lambda _: found[next(numbers)], array)


def merged_by_axis(array, axes, combine):
    for axis in axes:
        pieces = gathered_once(array, axis)
        array = jax.tree.map(lambda part: part[0], pieces)
        for k in range(1, lax.axis_size(axis)):
            array = combine(array, jax.tree.map(lambda part: part[k], pieces))
    return array


def from_everyone(array, axis):
    copies = jnp.broadcast_to(array, (lax.axis_size(axis), *array.shape))
    return lax.all_to_all(copies, axis, split_axis=0, concat_axis=0, tiled=True)


def taken_together(array, axis):
    everything = from_everyone(array, axis)
    return jnp.sum(everything, axis=0)


def one_axis_at_a_time(array, axes):
    return functools.reduce(lax.psum, axes, array)


def score_block(moving, codebook):
    return lax.dot_general(
        moving, codebook, (((1,), (1,)), ((), ())), preferred_element_type=jnp.float32
    )


def merge_stats(earlier, later):
    new_high = jnp.maximum(earlier[0], later[0])
    new_total = earlier[1] * jnp.exp(earlier[0] - new_high) + later[1] * jnp.exp(
        later[0] - new_high
    )
    return (new_high, new_total)


def entropy_part(usage, frames_total):
    mean_use = usage / frames_total
    return -jnp.sum(mean_use * jnp.log(mean_use + 1e-07))


def per_device(frames, codebook):
    frame_rows = frames[0]
    shard_rows = frame_rows.shape[0]
    cycle_size = lax.axis_size(BLK)
    cycle_index = lax.axis_index(BLK)
    group_rows = shard_rows * cycle_size
    scores = score_block(lax.all_gather(frame_rows, BLK, axis=0, tiled=True), codebook)
    local_high = jnp.max(scores, axis=1)
    local_total = jnp.sum(jnp.exp(scores - local_high[:, None]), axis=1)
    row_high, row_total = merged_by_axis((local_high, local_total), BLK, merge_stats)
    lse_all = row_high + jnp.log(row_total)
    lse_own = lax.dynamic_slice_in_dim(lse_all, cycle_index * shard_rows, shard_rows, 0)
    usage_part = jnp.sum(jnp.exp(scores - lse_all[:, None]), axis=0)
    frames_total = group_rows * lax.axis_size("rep")
    usage = taken_together(usage_part, "rep")
    entropy = one_axis_at_a_time(entropy_part(usage, frames_total), BLK)
    return (lse_own[None, :], usage, entropy)


def solution(mesh):
    split = Mesh(
        mesh.devices.reshape(4, 8, 2, 2, mesh.shape["rep"]),
        ("blk_0", "blk_1", "blk_2", "blk_3", "rep"),
    )
    return jax.shard_map(
        per_device,
        mesh=split,
        in_specs=(P("rep", BLK, None), P(BLK, None)),
        out_specs=(P("rep", BLK), P(BLK), P()),
        check_vma=False,
    )
```

profile of v0, /device:TPU:1, one launch (start us, length us, event | category | flops | bytes accessed | tf_op | source)
XLA Modules:
  0.0 265.5 jit_solution(1867115252379620708)
XLA Ops:
  7.2 0.0 copy-start
  7.2 0.0 all-gather.11.cloned.1.call-start
  7.2 0.7 all-gather.11.cloned.1.call-update
  7.9 128.6 %all-gather.11.cloned.1.call-done = bf16[1,6144,384]{2,1,0:T(8,128)(2,1)} async-done(((bf16[1,48,384]{2,1,0:T(8,128)(2,1)}), bf16[1,6144,384]{2,1,0:T(8,128)(2,1)}) %all-gather.11.cloned.1.call-update) | async-done | bytes 4718608 | tf_op jit(solution)/shard_map/all_gather | solution.py:76
  136.5 0.0 copy-done
  136.5 14.0 %fusion.52 = (f32[6144]{0:T(1024)S(1)}, f32[6144,1024]{0,1:T(8,128)}) fusion(bf16[1024,384]{1,0:T(8,128)(2,1)S(1)} %copy-done, bf16[1,6144,384]{2,1,0:T(8,128)(2,1)} %all-gather.11.cloned.1.call-done), kind=kOutput, calls=%fused_computation.87 | convolution fusion | flops 4838123520 | bytes 30695424 | tf_op jit(solution)/shard_map/dot_general | solution.py:52
  150.5 0.0 copy-start.1
  150.5 10.4 %exponential_reduce_fusion.1 = f32[6144]{0:T(1024)S(1)} fusion(f32[6144,1024]{0,1:T(8,128)} %get-tuple-element.14, f32[6144]{0:T(1024)S(1)} %get-tuple-element.13), kind=kLoop, calls=%fused_computation.1 | loop fusion | flops 12576768 | bytes 25214976 | tf_op jit(solution)/shard_map/reduce_sum | solution.py:78
  161.0 10.2 %all-gather.5 = f32[4,2,6144]{2,1,0:T(2,128)S(1)} all-gather(f32[1,2,6144]{2,1,0:T(2,128)S(1)} %maximum_bitcast_fusion), channel_id=3, replica_groups=mesh['blk_0'=4,'blk_1'=8,'blk_2'=2,'blk_3'=2,'rep'=2] {'blk_0'}, dimensions={0}, use_global_device_ids=true | all-gather | bytes 245760 | tf_op jit(solution)/shard_map/all_gather | solution.py:19
  171.1 0.2 fusion.27
  171.4 19.0 %all-gather.6 = f32[8,2,6144]{2,1,0:T(2,128)S(1)} all-gather(f32[1,2,6144]{2,1,0:T(2,128)S(1)} %maximum_bitcast_fusion.1), channel_id=4, replica_groups=mesh['blk_0'=4,'blk_1'=8,'blk_2'=2,'blk_3'=2,'rep'=2] {'blk_1'}, dimensions={0}, use_global_device_ids=true | all-gather | bytes 442368 | tf_op jit(solution)/shard_map/all_gather | solution.py:19
  190.5 0.6 fusion.6
  191.1 5.1 %all-gather.7 = f32[2,2,6144]{2,1,0:T(2,128)S(1)} all-gather(f32[1,2,6144]{2,1,0:T(2,128)S(1)} %maximum_bitcast_fusion.2), channel_id=5, replica_groups=mesh['blk_0'=4,'blk_1'=8,'blk_2'=2,'blk_3'=2,'rep'=2] {'blk_2'}, dimensions={0}, use_global_device_ids=true | all-gather | bytes 147456 | tf_op jit(solution)/shard_map/all_gather | solution.py:19
  196.2 0.1 fusion.3
  196.4 11.4 %all-gather.8 = f32[2,2,6144]{2,1,0:T(2,128)S(1)} all-gather(f32[1,2,6144]{2,1,0:T(2,128)S(1)} %maximum_bitcast_fusion.3), channel_id=6, replica_groups=mesh['blk_0'=4,'blk_1'=8,'blk_2'=2,'blk_3'=2,'rep'=2] {'blk_3'}, dimensions={0}, use_global_device_ids=true | all-gather | bytes 147456 | tf_op jit(solution)/shard_map/all_gather | solution.py:19
  207.8 0.1 fusion.51
  207.9 0.0 copy-done.1
  207.9 3.8 %exponential_reduce_fusion = f32[1024]{0:T(1024)S(1)} fusion(f32[6144,1024]{0,1:T(8,128)S(1)} %copy-done.1, f32[6144]{0:T(1024)S(1)} %log_add_fusion), kind=kLoop, calls=%fused_computation | loop fusion | flops 12581888 | bytes 25194496 | tf_op jit(solution)/shard_map/reduce_sum | solution.py:82
  211.7 0.6 broadcast_in_dim.9
  212.3 3.2 %all-to-all-start = ((f32[2,1,1024]{2,1,0:T(1,128)}), f32[2,1,1024]{2,1,0:T(1,128)S(1)}, u32[]{:S(2)}, u32[]{:S(2)}) async-start(f32[2,1,1024]{2,1,0:T(1,128)} %broadcast_in_dim.9), calls=%async_computation | async-start | bytes 16384 | tf_op jit(solution)/shard_map/all_to_all | solution.py:39
  215.6 2.6 all-to-all-done
  218.2 0.0 copy-start.2
  218.3 0.6 multiply_reduce_fusion
  219.5 8.9 %psum.28 = f32[]{:T(128)} all-reduce(f32[]{:T(128)S(6)} %neg.3), channel_id=1, replica_groups=mesh['blk_0'=4,'blk_1'=8,'blk_2'=2,'blk_3'=2,'rep'=2] {'blk_0'}, use_global_device_ids=true, to_apply=%region_5.6 | all-reduce | flops 1 | bytes 8 | tf_op jit(solution)/shard_map/psum | solution.py:48
  228.5 12.5 %psum.29 = f32[]{:T(128)} all-reduce(f32[]{:T(128)} %psum.28), channel_id=1, replica_groups=mesh['blk_0'=4,'blk_1'=8,'blk_2'=2,'blk_3'=2,'rep'=2] {'blk_1'}, use_global_device_ids=true, to_apply=%region_6.7 | all-reduce | flops 1 | bytes 8 | tf_op jit(solution)/shard_map/psum | solution.py:48
  241.0 5.9 %psum.30 = f32[]{:T(128)} all-reduce(f32[]{:T(128)} %psum.29), channel_id=1, replica_groups=mesh['blk_0'=4,'blk_1'=8,'blk_2'=2,'blk_3'=2,'rep'=2] {'blk_2'}, use_global_device_ids=true, to_apply=%region_7.8 | all-reduce | flops 1 | bytes 8 | tf_op jit(solution)/shard_map/psum | solution.py:48
  246.9 0.6 dynamic-slice_bitcast_fusion
  247.5 11.2 %psum.31 = f32[]{:T(128)} all-reduce(f32[]{:T(128)} %psum.30), channel_id=1, replica_groups=mesh['blk_0'=4,'blk_1'=8,'blk_2'=2,'blk_3'=2,'rep'=2] {'blk_3'}, use_global_device_ids=true, to_apply=%region_8.9 | all-reduce | flops 1 | bytes 8 | tf_op jit(solution)/shard_map/psum | solution.py:48
  258.6 0.0 copy-done.2
  (6 shorter events, 0.2 us)
Async XLA Ops:
  7.2 129.3 %copy-start = (bf16[1024,384]{1,0:T(8,128)(2,1)S(1)}, bf16[1024,384]{1,0:T(8,128)(2,1)}, u32[]{:S(2)}) copy-start(bf16[1024,384]{1,0:T(8,128)(2,1)} %param.3) | copy-start | bytes 2359300
  7.2 129.3 %all-gather.11.cloned.1.call-start = ((), (), s32[]{:S(2)}) async-start(), calls=%async_computation.1 | async-start | bytes 4755456 | tf_op jit(solution)/shard_map/all_gather | solution.py:76
  150.5 57.4 %copy-start.1 = (f32[6144,1024]{0,1:T(8,128)S(1)}, f32[6144,1024]{0,1:T(8,128)}, u32[]{:S(2)}) copy-start(f32[6144,1024]{0,1:T(8,128)} %get-tuple-element.14) | copy-start | bytes 75497472
  212.3 5.9 %all-to-all-start = ((f32[2,1,1024]{2,1,0:T(1,128)}), f32[2,1,1024]{2,1,0:T(1,128)S(1)}, u32[]{:S(2)}, u32[]{:S(2)}) async-start(f32[2,1,1024]{2,1,0:T(1,128)} %broadcast_in_dim.9), calls=%async_computation | async-start | bytes 16384 | tf_op jit(solution)/shard_map/all_to_all | solution.py:39
  218.2 40.4 %copy-start.2 = (f32[1024]{0:T(1024)}, f32[1024]{0:T(1024)S(1)}, u32[]{:S(2)}) copy-start(f32[1024]{0:T(1024)S(1)} %reduce_sum.38) | copy-start | bytes 12292
Sparse Core Ops, SparseCore 0:
  11.9 124.5 all-gather.10
where the time goes:
time: 266 us; the launch traced here: 265 us
  waiting for transfers between devices  132 us (50%)
  blocking collectives  84.3 us (32%)
  other arithmetic  16 us (6%)
  between operations  14.8 us (6%)
  matrix products  14 us (5%)
  starting transfers between devices  3.26 us (1%)
    all_gather x1, waiting for transfers between devices, per_device(): lax.all_gather(frame_rows, BLK, axis=0, tiled=True)  129 us
    all_gather x4, blocking collectives, gathered_once(): both, at, found = (lax.all_gather(jnp.concatenate(lines), axis), 0, {})  45.7 us
    psum x4, blocking collectives, one_axis_at_a_time(): return functools.reduce(lax.psum, axes, array)  38.5 us
    dot_general x1, matrix products, score_block(): lax.dot_general(moving, codebook, (((1,), (1,)), ((), ())), preferred_ele...  14 us
    reduce_sum x1, other arithmetic, per_device(): local_total = jnp.sum(jnp.exp(scores - local_high[:, None]), axis=1)  10.4 us
  transfers between devices with their start and end apart: 2, of which 2 were waited for; matrix products, arithmetic and copies ran while one was open for 0% of the time, Pallas kernels for 0%

commit v1 on v0

--- a/solution.py
+++ b/solution.py
@@ -6,6 +6,13 @@
 from jax.sharding import PartitionSpec as P
 
 BLK = ("blk_0", "blk_1", "blk_2", "blk_3")
+
+
+def gather_over(shard, axis, along):
+    devices = lax.axis_size(axis)
+    blocks = jnp.stack([shard for _ in range(devices)])
+    blocks = lax.all_to_all(blocks, axis, split_axis=0, concat_axis=0)
+    return jnp.concatenate(blocks, axis=along)
 
 
 def gathered_once(array, axis):
@@ -73,7 +80,7 @@
     cycle_size = lax.axis_size(BLK)
     cycle_index = lax.axis_index(BLK)
     group_rows = shard_rows * cycle_size
-    scores = score_block(lax.all_gather(frame_rows, BLK, axis=0, tiled=True), codebook)
+    scores = score_block(gather_over(frame_rows, BLK, 0), codebook)
     local_high = jnp.max(scores, axis=1)
     local_total = jnp.sum(jnp.exp(scores - local_high[:, None]), axis=1)
     row_high, row_total = merged_by_axis((local_high, local_total), BLK, merge_stats)

time: 266 us -> 247 us (0.929)
  waiting for transfers between devices: 132 us -> 2.64 us
  blocking collectives: 84.3 us -> 209 us
  between operations: 14.8 us -> 1.39 us
    all_gather x1 -> x0, waiting for transfers between devices: 129 us -> none  [per_device(): lax.all_gather(frame_rows, BLK, axis=0, tiled=True)]
    all_to_all x0 -> x1, blocking collectives: none -> 126 us  [gather_over(): blocks = lax.all_to_all(blocks, axis, split_axis=0, concat_axis=0)]
  transfers between devices with their start and end apart: 2 -> 1, of which waited for: 2 -> 1; matrix products, arithmetic and copies ran while one was open for 0% -> 0% of each run, Pallas kernels for 0% -> 0%
where the time goes in v1:
time: 247 us
  blocking collectives  209 us (85%)
  other arithmetic  16 us (6%)
  matrix products  11.8 us (5%)
  starting transfers between devices  3.22 us (1%)
  waiting for transfers between devices  2.64 us (1%)
  local copies, waits for them, and re-layouts  2.53 us (1%)
    all_to_all x1, blocking collectives, gather_over(): blocks = lax.all_to_all(blocks, axis, split_axis=0, concat_axis=0)  126 us
    all_gather x4, blocking collectives, gathered_once(): both, at, found = (lax.all_gather(jnp.concatenate(lines), axis), 0, {})  45.5 us
    psum x4, blocking collectives, one_axis_at_a_time(): return functools.reduce(lax.psum, axes, array)  37.3 us
    dot_general x1, matrix products, score_block(): lax.dot_general(moving, codebook, (((1,), (1,)), ((), ())), preferred_ele...  11.8 us
    reduce_sum x1, other arithmetic, per_device(): local_total = jnp.sum(jnp.exp(scores - local_high[:, None]), axis=1)  10.4 us
  transfers between devices with their start and end apart: 1, of which 1 were waited for; matrix products, arithmetic and copies ran while one was open for 0% of the time, Pallas kernels for 0%

profile of v1, /device:TPU:1, one launch (start us, length us, event | category | flops | bytes accessed | tf_op | source)
XLA Modules:
  0.0 246.8 jit_solution(9040524913679452634)
XLA Ops:
  0.6 0.0 copy-start
  0.6 1.2 stack.3
  1.9 126.3 %all_to_all.11 = bf16[128,48,384]{2,1,0:T(8,128)(2,1)S(1)} all-to-all(bf16[128,48,384]{2,1,0:T(8,128)(2,1)S(1)} %stack.3), channel_id=1, replica_groups=mesh['blk_0'=4,'blk_1'=8,'blk_2'=2,'blk_3'=2,'rep'=2] {'blk_0','blk_1','..., dimensions={0} | all-to-all | bytes 9437184 | tf_op jit(solution)/shard_map/all_to_all | solution.py:14
  128.2 0.0 copy-done
  128.2 11.8 %fusion.50 = (f32[6144]{0:T(1024)S(1)}, f32[6144,1024]{0,1:T(8,128)}) fusion(bf16[6144,384]{1,0:T(8,128)(2,1)S(1)} %bitcast.274, bf16[1024,384]{1,0:T(8,128)(2,1)S(1)} %copy-done), kind=kOutput, calls=%fused_computation.85 | convolution fusion | flops 4838123520 | bytes 30695424 | tf_op jit(solution)/shard_map/dot_general | solution.py:59
  140.1 0.0 copy-start.1
  140.1 10.4 %exponential_reduce_fusion.1 = f32[6144]{0:T(1024)S(1)} fusion(f32[6144,1024]{0,1:T(8,128)} %get-tuple-element.14, f32[6144]{0:T(1024)S(1)} %get-tuple-element.13), kind=kLoop, calls=%fused_computation.1 | loop fusion | flops 12576768 | bytes 25214976 | tf_op jit(solution)/shard_map/reduce_sum | solution.py:85
  150.5 9.4 %all-gather.4 = f32[4,2,6144]{2,1,0:T(2,128)S(1)} all-gather(f32[1,2,6144]{2,1,0:T(2,128)S(1)} %maximum_bitcast_fusion), channel_id=2, replica_groups=mesh['blk_0'=4,'blk_1'=8,'blk_2'=2,'blk_3'=2,'rep'=2] {'blk_0'}, dimensions={0}, use_global_device_ids=true | all-gather | bytes 245760 | tf_op jit(solution)/shard_map/all_gather | solution.py:26
  159.9 0.2 fusion.25
  160.2 19.4 %all-gather.5 = f32[8,2,6144]{2,1,0:T(2,128)S(1)} all-gather(f32[1,2,6144]{2,1,0:T(2,128)S(1)} %maximum_bitcast_fusion.1), channel_id=3, replica_groups=mesh['blk_0'=4,'blk_1'=8,'blk_2'=2,'blk_3'=2,'rep'=2] {'blk_1'}, dimensions={0}, use_global_device_ids=true | all-gather | bytes 442368 | tf_op jit(solution)/shard_map/all_gather | solution.py:26
  179.6 0.6 fusion.4
  180.2 5.1 %all-gather.6 = f32[2,2,6144]{2,1,0:T(2,128)S(1)} all-gather(f32[1,2,6144]{2,1,0:T(2,128)S(1)} %maximum_bitcast_fusion.2), channel_id=4, replica_groups=mesh['blk_0'=4,'blk_1'=8,'blk_2'=2,'blk_3'=2,'rep'=2] {'blk_2'}, dimensions={0}, use_global_device_ids=true | all-gather | bytes 147456 | tf_op jit(solution)/shard_map/all_gather | solution.py:26
  185.3 0.1 fusion.1
  185.5 11.6 %all-gather.7 = f32[2,2,6144]{2,1,0:T(2,128)S(1)} all-gather(f32[1,2,6144]{2,1,0:T(2,128)S(1)} %maximum_bitcast_fusion.3), channel_id=5, replica_groups=mesh['blk_0'=4,'blk_1'=8,'blk_2'=2,'blk_3'=2,'rep'=2] {'blk_3'}, dimensions={0}, use_global_device_ids=true | all-gather | bytes 147456 | tf_op jit(solution)/shard_map/all_gather | solution.py:26
  197.1 0.1 fusion.49
  197.2 0.0 copy-done.1
  197.2 3.8 %exponential_reduce_fusion = f32[1024]{0:T(1024)S(1)} fusion(f32[6144,1024]{0,1:T(8,128)S(1)} %copy-done.1, f32[6144]{0:T(1024)S(1)} %log_add_fusion), kind=kLoop, calls=%fused_computation | loop fusion | flops 12581888 | bytes 25194496 | tf_op jit(solution)/shard_map/reduce_sum | solution.py:89
  201.1 0.6 broadcast_in_dim.9
  201.7 3.2 %all-to-all-start.1 = ((f32[2,1,1024]{2,1,0:T(1,128)}), f32[2,1,1024]{2,1,0:T(1,128)S(1)}, u32[]{:S(2)}, u32[]{:S(2)}) async-start(f32[2,1,1024]{2,1,0:T(1,128)} %broadcast_in_dim.9), calls=%async_computation.1 | async-start | bytes 16384 | tf_op jit(solution)/shard_map/all_to_all | solution.py:46
  204.9 2.6 %all-to-all-done.1 = f32[2,1,1024]{2,1,0:T(1,128)S(1)} async-done(((f32[2,1,1024]{2,1,0:T(1,128)}), f32[2,1,1024]{2,1,0:T(1,128)S(1)}, u32[]{:S(2)}, u32[]{:S(2)}) %all-to-all-start.1) | async-done | bytes 8224 | tf_op jit(solution)/shard_map/all_to_all | solution.py:46
  207.6 0.0 copy-start.2
  207.6 0.6 multiply_reduce_fusion
  208.8 7.3 %psum.28 = f32[]{:T(128)} all-reduce(f32[]{:T(128)S(6)} %neg.3), channel_id=1, replica_groups=mesh['blk_0'=4,'blk_1'=8,'blk_2'=2,'blk_3'=2,'rep'=2] {'blk_0'}, use_global_device_ids=true, to_apply=%region_5.6 | all-reduce | flops 1 | bytes 8 | tf_op jit(solution)/shard_map/psum | solution.py:55
  216.1 13.0 %psum.29 = f32[]{:T(128)} all-reduce(f32[]{:T(128)} %psum.28), channel_id=1, replica_groups=mesh['blk_0'=4,'blk_1'=8,'blk_2'=2,'blk_3'=2,'rep'=2] {'blk_1'}, use_global_device_ids=true, to_apply=%region_6.7 | all-reduce | flops 1 | bytes 8 | tf_op jit(solution)/shard_map/psum | solution.py:55
  229.1 5.9 %psum.30 = f32[]{:T(128)} all-reduce(f32[]{:T(128)} %psum.29), channel_id=1, replica_groups=mesh['blk_0'=4,'blk_1'=8,'blk_2'=2,'blk_3'=2,'rep'=2] {'blk_2'}, use_global_device_ids=true, to_apply=%region_7.8 | all-reduce | flops 1 | bytes 8 | tf_op jit(solution)/shard_map/psum | solution.py:55
  235.0 0.6 dynamic-slice_bitcast_fusion
  235.6 11.2 %psum.31 = f32[]{:T(128)} all-reduce(f32[]{:T(128)} %psum.30), channel_id=1, replica_groups=mesh['blk_0'=4,'blk_1'=8,'blk_2'=2,'blk_3'=2,'rep'=2] {'blk_3'}, use_global_device_ids=true, to_apply=%region_8.9 | all-reduce | flops 1 | bytes 8 | tf_op jit(solution)/shard_map/psum | solution.py:55
  246.8 0.0 copy-done.2
  (6 shorter events, 0.2 us)
Async XLA Ops:
  0.6 127.6 %copy-start = (bf16[1024,384]{1,0:T(8,128)(2,1)S(1)}, bf16[1024,384]{1,0:T(8,128)(2,1)}, u32[]{:S(2)}) copy-start(bf16[1024,384]{1,0:T(8,128)(2,1)} %param.3) | copy-start | bytes 2359300
  140.1 57.2 %copy-start.1 = (f32[6144,1024]{0,1:T(8,128)S(1)}, f32[6144,1024]{0,1:T(8,128)}, u32[]{:S(2)}) copy-start(f32[6144,1024]{0,1:T(8,128)} %get-tuple-element.14) | copy-start | bytes 75497472
  201.7 5.9 %all-to-all-start.1 = ((f32[2,1,1024]{2,1,0:T(1,128)}), f32[2,1,1024]{2,1,0:T(1,128)S(1)}, u32[]{:S(2)}, u32[]{:S(2)}) async-start(f32[2,1,1024]{2,1,0:T(1,128)} %broadcast_in_dim.9), calls=%async_computation.1 | async-start | bytes 16384 | tf_op jit(solution)/shard_map/all_to_all | solution.py:46
  207.6 39.2 %copy-start.2 = (f32[1024]{0:T(1024)}, f32[1024]{0:T(1024)S(1)}, u32[]{:S(2)}) copy-start(f32[1024]{0:T(1024)S(1)} %reduce_sum.38) | copy-start | bytes 12292
